TPU v7x, 512 devices: a whole 4x8x8 slice. The times are simulated.
512 devices in a mesh: expert: 64 (over z_lo, y, x), shard: 8 (over z_hi, core).
Axes of the slice: x: 4, y: 8, z: 8 (z_hi: 4, z_lo: 2; z = z_hi * 2 + z_lo), core: 2. Of those that a mesh axis runs over, the one named last changes fastest.
Arguments:
- w_gate: float32 [64, 2048, 1024], P('expert', 'shard'), may hold values from -0.125 to 0.125
- avg_gate: float32 [64, 2048, 1024], P('expert', 'shard'), may hold values from -0.125 to 0.125
- w_up: float32 [64, 2048, 1024], P('expert', 'shard'), may hold values from -0.125 to 0.125
- avg_up: float32 [64, 2048, 1024], P('expert', 'shard'), may hold values from -0.125 to 0.125
- mix_share: float32 [64], P('expert'), may hold values from 0.2 to 0.8
- router_weight: float32 [2048, 64], P('shard', 'expert'), may hold values from -0.125 to 0.125
- router_gain: float32 [2048], P('shard'), may hold values from 0.25 to 1.75
Outputs:
- serve_gate: bfloat16 [64, 1024, 2048], P('expert')
- serve_up: bfloat16 [64, 1024, 2048], P('expert')
- serve_router: bfloat16 [2048, 64], replicated
All inputs are finite; a program needn't handle non-finite values.
Results may differ from a plain program's by a relative error of at most 0.001.
Values may be sent and summed in bfloat16 or wider, within the bound.
No kernel may reach another device: no remote copies, remote signals or barrier semaphores. Data moves between devices by JAX's collectives and lax.ppermute only.
A program may use at most 64 MiB of HBM per device.

v0:
```python
import functools

import jax
import jax.numpy as jnp
from jax import lax
from jax.experimental import pallas as pl
from jax.experimental.pallas import tpu as pltpu
from jax.sharding import Mesh
from jax.sharding import PartitionSpec as P


BF16 = jnp.bfloat16
WIDTH = 256
HEAD = 256
EXPERT = ("zlo", "y", "x")
SHARD = ("zhi", "core")
ANY = pl.BlockSpec(memory_space=pl.ANY)
HBM = pl.BlockSpec(memory_space=pltpu.HBM)
VMEM = pl.BlockSpec(memory_space=pltpu.VMEM)
SMEM = pl.BlockSpec(memory_space=pltpu.SMEM)
GATE, UP = 0, 1
AHEAD = -1


def mix_kernel(first, size, share_ref, w, avg, before, out, whole, buf, sems):
    chunks = [(col, min(WIDTH, size - col)) for col in range(0, size, WIDTH)]

    def copies(k):
        col, wide = chunks[k]
        return [
            pltpu.make_async_copy(src.at[:, pl.ds(first + col, wide)], buf.at[i, k, :, pl.ds(0, wide)], sems.at[i, k])
            for i, src in enumerate((w, avg))
        ]

    for k in range(len(chunks)):
        for c in copies(k):
            c.start()
    share = share_ref[0]
    rest = 1.0 - share
    for k, (col, wide) in enumerate(chunks):
        for c in copies(k):
            c.wait()
        fresh = share * buf[0, k, :, :wide] + rest * buf[1, k, :, :wide]
        turned = fresh.astype(BF16).T
        out[pl.ds(col, wide), :] = turned
        whole[pl.ds(before.shape[0] + col, wide), :] = turned
    whole[pl.ds(0, before.shape[0]), :] = before[...]


def mark_kernel(out):
    out[...] = jnp.zeros(out.shape, out.dtype)


def marked():
    return pl.pallas_call(
        mark_kernel,
        out_shape=pltpu.VMEM((8, 128), jnp.float32),
        out_specs=VMEM,
        compiler_params=pltpu.CompilerParams(vmem_limit_bytes=1 << 20),
        cost_estimate=pl.CostEstimate(flops=1 << 34, bytes_accessed=1 << 24, transcendentals=0),
        name="mark",
    )()


def near_kernel(share_ref, w, avg, mark, out):
    share = share_ref[0]
    rest = 1.0 - share
    for col in range(0, w.shape[1], WIDTH):
        cols = pl.ds(col, WIDTH)
        fresh = share * w[:, cols] + rest * avg[:, cols]
        out[cols, :] = fresh.astype(BF16).T


def mixed_near(share, w, avg, mark):
    rows, columns = w.shape
    return pl.pallas_call(
        near_kernel,
        out_shape=pltpu.VMEM((columns, rows), BF16),
        in_specs=[SMEM] + [VMEM] * 3,
        out_specs=VMEM,
        compiler_params=pltpu.CompilerParams(vmem_limit_bytes=12 << 20),
        cost_estimate=pl.CostEstimate(flops=4 * rows * columns, bytes_accessed=10 * rows * columns, transcendentals=0),
        name="mix",
    )(share, *(pltpu.with_memory_space_constraint(x, pltpu.VMEM) for x in (w, avg, mark)))


def mixed(share, w, avg, first, size, before):
    rows = w.shape[0]
    w, avg = (pltpu.with_memory_space_constraint(x, pltpu.HBM) for x in (w, avg))
    chunks = -(-size // WIDTH)
    return pl.pallas_call(
        functools.partial(mix_kernel, first, size),
        out_shape=(pltpu.VMEM((size, rows), BF16), pltpu.VMEM((before.shape[0] + size, rows), BF16)),
        in_specs=[SMEM, HBM, HBM, VMEM],
        out_specs=(VMEM, VMEM),
        scratch_shapes=[
            pltpu.VMEM((2, chunks, rows, WIDTH), jnp.float32),
            pltpu.SemaphoreType.DMA((2, chunks)),
        ],
        compiler_params=pltpu.CompilerParams(vmem_limit_bytes=12 << 20),
        cost_estimate=pl.CostEstimate(flops=4 * rows * size, bytes_accessed=10 * rows * size, transcendentals=0),
        name="mix",
    )(share, w, avg, pltpu.with_memory_space_constraint(before, pltpu.VMEM))


def join_kernel(a_ref, b_ref, out_ref):
    rows = a_ref.shape[0]
    out_ref[pl.ds(0, rows), :] = a_ref[...]
    out_ref[pl.ds(rows, b_ref.shape[0]), :] = b_ref[...]


def joined(a, b):
    shape = (a.shape[0] + b.shape[0], a.shape[1])
    a, b = (pltpu.with_memory_space_constraint(x, pltpu.VMEM) for x in (a, b))
    return pl.pallas_call(
        join_kernel,
        out_shape=pltpu.VMEM(shape, BF16),
        in_specs=[VMEM, VMEM],
        out_specs=VMEM,
        compiler_params=pltpu.CompilerParams(vmem_limit_bytes=4 << 20),
        cost_estimate=pl.CostEstimate(flops=shape[0] * shape[1], bytes_accessed=4 * shape[0] * shape[1], transcendentals=0),
        name="join",
    )(a, b)


def place_kernel(counts, by, *refs):
    outs, sems = refs[-3:-1], refs[-1]
    width = refs[0].shape[1]
    chips = lax.axis_size("zhi")
    chip, core = lax.axis_index("zhi"), lax.axis_index("core")
    sign = AHEAD * (1 - 2 * lax.axis_index("zlo"))
    copies = []
    entries = iter(by)
    for ref, count in zip(refs, counts):
        row = 0
        for _ in range(count):
            which, start, size, step, other = next(entries)
            side = other - 2 if other > 1 else 1 - core if other else core
            owner = lax.rem(chip + chips - step * sign, chips) * 2 + side
            cols = pl.ds(pl.multiple_of(owner * width, width), width)
            piece = ref.at[pl.ds(row, size), :]
            row += size
            copies.append(pltpu.make_async_copy(piece, outs[which].at[pl.ds(start, size), cols], sems.at[len(copies)]))
    for c in copies:
        c.start()
    for c in copies:
        c.wait()


def placed(outs, arrays, columns, rows):
    n = len(arrays)
    by = tuple(p for _, pieces in arrays for p in pieces)
    counts = tuple(len(pieces) for _, pieces in arrays)
    arrays = [pltpu.with_memory_space_constraint(a, pltpu.VMEM) for a, _ in arrays]
    width = arrays[0].shape[1]
    total = sum(p[2] for p in by)
    out = jax.ShapeDtypeStruct((rows, columns), BF16)
    extra = () if outs is None else tuple(outs)
    return pl.pallas_call(
        functools.partial(place_kernel, counts, by),
        out_shape=(out, out),
        in_specs=[VMEM] * n + [ANY] * len(extra),
        out_specs=(ANY, ANY),
        input_output_aliases={n + i: i for i in range(len(extra))},
        scratch_shapes=[pltpu.SemaphoreType.DMA((len(by),))],
        compiler_params=pltpu.CompilerParams(vmem_limit_bytes=12 << 20),
        cost_estimate=pl.CostEstimate(flops=2 * total * width, bytes_accessed=4 * total * width, transcendentals=0),
        name="place",
    )(*arrays, *extra)


def order_kernel(nxy, nz, in_ref, out_ref, wide):
    lanes = in_ref.shape[1]
    wide[...] = in_ref[...].astype(jnp.float32)
    column = in_ref.shape[0] // nxy
    for z in range(nz):
        for j in range(column // nz):
            rows = wide[pl.ds(z * (column // nz) + j, nxy, stride=column), :]
            out_ref[pl.ds(z * nxy, nxy), pl.ds(j * lanes, lanes)] = rows.astype(BF16)


def ordered(part, nxy, nz):
    rows, lanes = part.shape
    experts = nxy * nz
    return pl.pallas_call(
        functools.partial(order_kernel, nxy, nz),
        out_shape=jax.ShapeDtypeStruct((experts, rows * lanes // experts), BF16),
        in_specs=[VMEM],
        out_specs=VMEM,
        scratch_shapes=[
            pltpu.VMEM((rows, lanes), jnp.float32),
        ],
        compiler_params=pltpu.CompilerParams(vmem_limit_bytes=4 << 20),
        cost_estimate=pl.CostEstimate(flops=rows * lanes, bytes_accessed=4 * rows * lanes, transcendentals=0),
        name="order",
    )(part)


def spread(x, axes):
    n = lax.axis_size(axes)
    return lax.all_to_all(jnp.broadcast_to(x[None], (n, *x.shape)), axes, 0, 0, tiled=True)


def local(w_gate, avg_gate, w_up, avg_up, mix_share, router_weight, router_gain):
    chips = lax.axis_size("zhi")
    columns = w_gate.shape[1] * chips * lax.axis_size("core")
    rows = w_gate.shape[2]

    def moved(x, by):
        pairs = [
            (lo * chips + hi, lo * chips + (hi + (by if lo == 0 else -by)) % chips) for lo in range(2) for hi in range(chips)
        ]
        return lax.ppermute(x, ("zlo", "zhi"), pairs)

    def partner(x):
        return lax.ppermute(x, "core", [(0, 1), (1, 0)])

    def place(outs, *arrays):
        return placed(outs, arrays, columns, rows)

    def head(step, other):
        return ((GATE, 0, rows, step, other), (UP, 0, HEAD, step, other))

    def tail(step, other):
        return ((UP, HEAD, rows - HEAD, step, other),)

    mark = marked()
    start = mixed_near(mix_share, w_gate[0], avg_gate[0], mark)
    more, first = mixed(mix_share, w_up[0], avg_up[0], 0, HEAD, start)
    second, own = mixed(mix_share, w_up[0], avg_up[0], HEAD, rows - HEAD, first)
    a0 = moved(start, AHEAD)
    a1 = moved(more, AHEAD)
    a2 = moved(second, AHEAD)
    a1 = joined(a0, a1)
    c1 = moved(a1, AHEAD)
    c2 = moved(a2, AHEAD)
    f1 = moved(c1, AHEAD)
    f2 = moved(c2, AHEAD)

    nx, ny, nz = (lax.axis_size(a) for a in ("x", "y", "zlo"))
    part = (router_weight * router_gain[:, None]).astype(BF16).reshape(2, -1)
    lanes = part.shape[1]
    part = spread(part, ("zlo", "zhi", "core")).reshape(-1, lanes)
    part = spread(part, ("y", "x")).reshape(-1, lanes)
    serve_router = ordered(part, nx * ny, nz).T

    outs = place(None, (own, head(0, 0) + tail(0, 0)))
    d0 = partner(own)
    both = joined(a1, a2)
    d1 = partner(both)
    outs = place(outs, (a1, head(1, 0)), (a2, tail(1, 0)), (d0, head(0, 1) + tail(0, 1)), (d1, head(1, 1) + tail(1, 1)))
    both = joined(c1, c2)
    d2 = partner(both)
    outs = place(
        outs,
        (c1, head(2, 0)),
        (c2, tail(2, 0)),
        (d2, head(2, 1) + tail(2, 1)),
        (f1, head(3, 0)),
        (partner(f1), head(3, 1)),
    )
    last = lax.all_gather(f2, "core", axis=0, tiled=True)
    outs = place(outs, (last, tail(3, 2) + tail(3, 3)))
    return outs[0][None], outs[1][None], serve_router


def solution(mesh):
    devices = mesh.devices.reshape(2, 8, 4, 4, 2)
    split = Mesh(devices, EXPERT + SHARD)
    return jax.shard_map(
        local,
        mesh=split,
        in_specs=(
            P(EXPERT, SHARD, None),
            P(EXPERT, SHARD, None),
            P(EXPERT, SHARD, None),
            P(EXPERT, SHARD, None),
            P(EXPERT),
            P(SHARD, EXPERT),
            P(SHARD),
        ),
        out_specs=(P(EXPERT, None, None), P(EXPERT, None, None), P()),
        check_vma=False,
    )
```

profile of v0, /device:TPU:1, one launch (start us, length us, event | category | flops | bytes accessed | tf_op | source)
XLA Modules:
  0.0 125.9 jit_solution(13992979282545794005)
XLA Ops:
  0.6 0.0 copy-start
  0.6 0.0 copy-start.1
  1.5 0.4 copy-done
  1.9 0.3 copy-done.1
  2.2 0.2 mix.3.before
  2.4 11.5 %collective-permute-start.3 = (bf16[1024,256]{1,0:T(8,128)(2,1)S(1)}, bf16[1024,256]{1,0:T(8,128)(2,1)S(1)}, u32[]{:S(2)}, u32[]{:S(2)}) collective-permute-start(bf16[1024,256]{1,0:T(8,128)(2,1)S(1)} %mix.3.before), channel_id=1, source_target_pairs={{0,6},{2,0},{4,2},{6,4},{256,258},{258,260},{260,262},{262,256},{1... | collective-permute-start | bytes 1572872 | tf_op jit(solution)/shard_map/ppermute | solution.py:213
  13.9 1.2 mix.4
  15.1 0.0 copy-start.2
  15.1 0.0 copy-start.3
  15.1 2.2 %collective-permute-start.4 = (bf16[256,256]{1,0:T(8,128)(2,1)S(1)}, bf16[256,256]{1,0:T(8,128)(2,1)S(1)}, u32[]{:S(2)}, u32[]{:S(2)}) collective-permute-start(bf16[256,256]{1,0:T(8,128)(2,1)S(1)} %get-tuple-element.17), channel_id=1, source_target_pairs={{0,6},{2,0},{4,2},{6,4},{256,258},{258,260},{260,262},{262,256},{1... | collective-permute-start | bytes 393224 | tf_op jit(solution)/shard_map/ppermute | solution.py:213
  17.3 10.0 %collective-permute-done.4.b_ref = bf16[256,256]{1,0:T(8,128)(2,1)S(1)} collective-permute-done((bf16[256,256]{1,0:T(8,128)(2,1)S(1)}, bf16[256,256]{1,0:T(8,128)(2,1)S(1)}, u32[]{:S(2)}, u32[]{:S(2)}) %collective-permute-start.4) | collective-permute-done | bytes 131104 | tf_op jit(solution)/shard_map/ppermute | solution.py:213
  27.3 0.0 collective-permute-done.3.a_ref
  27.3 6.2 %collective-permute-start.5 = (bf16[1280,256]{1,0:T(8,128)(2,1)S(1)}, bf16[1280,256]{1,0:T(8,128)(2,1)S(1)}, u32[]{:S(2)}, u32[]{:S(2)}) collective-permute-start(bf16[1280,256]{1,0:T(8,128)(2,1)S(1)} %join.3.a_ref.refs_0_), channel_id=1, source_target_pairs={{0,6},{2,0},{4,2},{6,4},{256,258},{258,260},{260,262},{262,256},{1... | collective-permute-start | bytes 1966088 | tf_op jit(solution)/shard_map/ppermute | solution.py:213
  33.5 2.5 %mix.5 = (bf16[768,256]{1,0:T(8,128)(2,1)S(1)}, bf16[2048,256]{1,0:T(8,128)(2,1)}) custom-call(f32[1]{0:T(128)S(6)} %copy.22.share_ref, f32[256,1024]{1,0:T(8,128)} %bitcast.17, f32[256,1024]{1,0:T(8,128)} %bitcast.19, bf16[1280,256]{1,0:T(8,128)(2,1)S(1)} %get-tuple-element.15.before), custom_call_target="tpu_custom_call" | custom-call | flops 786432 | bytes 1966080 | tf_op jit(solution)/shard_map/mix/pallas_call | solution.py:91
  36.0 1.9 %collective-permute-start = (bf16[768,256]{1,0:T(8,128)(2,1)S(1)}, bf16[768,256]{1,0:T(8,128)(2,1)S(1)}, u32[]{:S(2)}, u32[]{:S(2)}) collective-permute-start(bf16[768,256]{1,0:T(8,128)(2,1)S(1)} %get-tuple-element.16), channel_id=1, source_target_pairs={{0,6},{2,0},{4,2},{6,4},{256,258},{258,260},{260,262},{262,256},{1... | collective-permute-start | bytes 1179656 | tf_op jit(solution)/shard_map/ppermute | solution.py:213
  38.0 16.5 %collective-permute-done.b_ref.refs_1_ = bf16[768,256]{1,0:T(8,128)(2,1)S(1)} collective-permute-done((bf16[768,256]{1,0:T(8,128)(2,1)S(1)}, bf16[768,256]{1,0:T(8,128)(2,1)S(1)}, u32[]{:S(2)}, u32[]{:S(2)}) %collective-permute-start) | collective-permute-done | bytes 393248 | tf_op jit(solution)/shard_map/ppermute | solution.py:213
  54.5 6.2 %collective-permute-start.1 = (bf16[768,256]{1,0:T(8,128)(2,1)S(1)}, bf16[768,256]{1,0:T(8,128)(2,1)S(1)}, u32[]{:S(2)}, u32[]{:S(2)}) collective-permute-start(bf16[768,256]{1,0:T(8,128)(2,1)S(1)} %collective-permute-done.b_ref.refs_1_), channel_id=1, source_target_pairs={{0,6},{2,0},{4,2},{6,4},{256,258},{258,260},{260,262},{262,256},{1... | collective-permute-start | bytes 1179656 | tf_op jit(solution)/shard_map/ppermute | solution.py:213
  60.7 0.0 collective-permute-done.5.a_ref.refs_0_
  60.7 1.9 %collective-permute-start.7 = (bf16[1280,256]{1,0:T(8,128)(2,1)S(1)}, bf16[1280,256]{1,0:T(8,128)(2,1)}, u32[]{:S(2)}, u32[]{:S(2)}) collective-permute-start(bf16[1280,256]{1,0:T(8,128)(2,1)S(1)} %collective-permute-done.5.a_ref.refs_0_), channel_id=1, source_target_pairs={{0,6},{2,0},{4,2},{6,4},{256,258},{258,260},{260,262},{262,256},{1... | collective-permute-start | bytes 1966088 | tf_op jit(solution)/shard_map/ppermute | solution.py:213
  62.7 4.6 %collective-permute-start.9 = (bf16[2048,256]{1,0:T(8,128)(2,1)}, bf16[2048,256]{1,0:T(8,128)(2,1)}, u32[]{:S(2)}, u32[]{:S(2)}) collective-permute-start(bf16[2048,256]{1,0:T(8,128)(2,1)} %get-tuple-element.18.refs_0_), channel_id=1, source_target_pairs={{0,1},{1,0},{2,3},{3,2},{4,5},{5,4},{6,7},{7,6},{8,9},{9,8},{10,11... | collective-permute-start | bytes 3145736 | tf_op jit(solution)/shard_map/ppermute | solution.py:216
  67.2 1.1 join.5
  68.3 1.9 %collective-permute-start.10 = (bf16[2048,256]{1,0:T(8,128)(2,1)}, bf16[2048,256]{1,0:T(8,128)(2,1)}, u32[]{:S(2)}, u32[]{:S(2)}) collective-permute-start(bf16[2048,256]{1,0:T(8,128)(2,1)} %join.5), channel_id=1, source_target_pairs={{0,1},{1,0},{2,3},{3,2},{4,5},{5,4},{6,7},{7,6},{8,9},{9,8},{10,11... | collective-permute-start | bytes 3145736 | tf_op jit(solution)/shard_map/ppermute | solution.py:216
  70.2 0.0 collective-permute-done.1.b_ref.refs_1_
  70.2 1.1 join.4
  71.3 4.5 %collective-permute-start.6 = (bf16[2048,256]{1,0:T(8,128)(2,1)}, bf16[2048,256]{1,0:T(8,128)(2,1)S(1)}, u32[]{:S(2)}, u32[]{:S(2)}) collective-permute-start(bf16[2048,256]{1,0:T(8,128)(2,1)} %join.4), channel_id=1, source_target_pairs={{0,1},{1,0},{2,3},{3,2},{4,5},{5,4},{6,7},{7,6},{8,9},{9,8},{10,11... | collective-permute-start | bytes 3145736 | tf_op jit(solution)/shard_map/ppermute | solution.py:216
  75.8 0.0 copy-done.2
  75.8 0.0 copy-done.3
  75.9 12.8 %all_to_all.10 = bf16[16,2,128]{2,1,0:T(2,128)(2,1)S(1)} all-to-all(bf16[16,2,128]{2,1,0:T(2,128)(2,1)S(1)} %broadcast_in_dim.27), channel_id=1, replica_groups=mesh['zlo'=2,'y'=8,'x'=4,'zhi'=4,'core'=2] {'zlo','zhi','core'}, dimensions={0} | all-to-all | bytes 16384 | tf_op jit(solution)/shard_map/all_to_all | solution.py:201
  88.7 0.7 broadcast_in_dim.29
  89.4 9.7 %all-to-all-start.1 = ((bf16[32,32,128]{2,1,0:T(8,128)(2,1)}), bf16[32,32,128]{2,1,0:T(8,128)(2,1)S(1)}, u32[]{:S(2)}, u32[]{:S(2)}) async-start(bf16[32,32,128]{2,1,0:T(8,128)(2,1)} %broadcast_in_dim.29), calls=%async_computation.1 | async-start | bytes 524288 | tf_op jit(solution)/shard_map/all_to_all | solution.py:201
  99.1 0.0 collective-permute-done.7.refs_3_
  99.1 2.8 %collective-permute-start.8 = (bf16[1280,256]{1,0:T(8,128)(2,1)}, bf16[1280,256]{1,0:T(8,128)(2,1)}, u32[]{:S(2)}, u32[]{:S(2)}) collective-permute-start(bf16[1280,256]{1,0:T(8,128)(2,1)} %collective-permute-done.7.refs_3_), channel_id=1, source_target_pairs={{0,1},{1,0},{2,3},{3,2},{4,5},{5,4},{6,7},{7,6},{8,9},{9,8},{10,11... | collective-permute-start | bytes 1966088 | tf_op jit(solution)/shard_map/ppermute | solution.py:216
  102.0 2.2 %collective-permute-start.2 = (bf16[768,256]{1,0:T(8,128)(2,1)S(1)}, bf16[768,256]{1,0:T(8,128)(2,1)}, u32[]{:S(2)}, u32[]{:S(2)}) collective-permute-start(bf16[768,256]{1,0:T(8,128)(2,1)S(1)} %collective-permute-done.1.b_ref.refs_1_), channel_id=1, source_target_pairs={{0,6},{2,0},{4,2},{6,4},{256,258},{258,260},{260,262},{262,256},{1... | collective-permute-start | bytes 1179656 | tf_op jit(solution)/shard_map/ppermute | solution.py:213
  104.2 2.2 %place.4 = (bf16[1024,2048]{1,0:T(8,128)(2,1)}, bf16[1024,2048]{1,0:T(8,128)(2,1)}) custom-call(bf16[2048,256]{1,0:T(8,128)(2,1)} %get-tuple-element.18.refs_0_), custom_call_target="tpu_custom_call" | custom-call | flops 1048576 | bytes 2097152 | tf_op jit(solution)/shard_map/place/pallas_call | solution.py:159
  106.4 4.0 %all-to-all-done.1 = bf16[32,32,128]{2,1,0:T(8,128)(2,1)S(1)} async-done(((bf16[32,32,128]{2,1,0:T(8,128)(2,1)}), bf16[32,32,128]{2,1,0:T(8,128)(2,1)S(1)}, u32[]{:S(2)}, u32[]{:S(2)}) %all-to-all-start.1) | async-done | bytes 262176 | tf_op jit(solution)/shard_map/all_to_all | solution.py:201
  110.4 1.0 order.1
  111.5 4.1 %collective-permute-done.2 = bf16[768,256]{1,0:T(8,128)(2,1)} collective-permute-done((bf16[768,256]{1,0:T(8,128)(2,1)S(1)}, bf16[768,256]{1,0:T(8,128)(2,1)}, u32[]{:S(2)}, u32[]{:S(2)}) %collective-permute-start.2) | collective-permute-done | bytes 393248 | tf_op jit(solution)/shard_map/ppermute | solution.py:213
  115.5 3.1 %all_gather.3.refs_0_ = bf16[1536,256]{1,0:T(8,128)(2,1)S(1)} all-gather(bf16[768,256]{1,0:T(8,128)(2,1)} %collective-permute-done.2), channel_id=1, replica_groups=mesh['zlo'=2,'y'=8,'x'=4,'zhi'=4,'core'=2] {'core'}, dimensions={0}, use_global_device_ids=true | all-gather | bytes 1179648 | tf_op jit(solution)/shard_map/all_gather | solution.py:262
  118.6 0.0 collective-permute-done.9.refs_2_
  118.6 0.0 collective-permute-done.10.refs_3_
  118.6 3.3 %place.5 = (bf16[1024,2048]{1,0:T(8,128)(2,1)}, bf16[1024,2048]{1,0:T(8,128)(2,1)}) custom-call(bf16[1280,256]{1,0:T(8,128)(2,1)S(1)} %join.3.a_ref.refs_0_, bf16[768,256]{1,0:T(8,128)(2,1)S(1)} %collective-permute-done.b_ref.refs_1_, bf16[2048,256]{1,0:T(8,128)(2,1)} %collective-permute-done.9.refs_2_, ...), custom_call_target="tpu_custom_call", output_to_operand_aliasing={{0}: (4, {}), {1}: (5, {})} | custom-call | flops 3145728 | bytes 6291456 | tf_op jit(solution)/shard_map/place/pallas_call | solution.py:159
  121.9 0.0 collective-permute-done.6.refs_2_
  121.9 0.0 collective-permute-done.8.refs_4_
  121.9 3.1 %place.6 = (bf16[1024,2048]{1,0:T(8,128)(2,1)}, bf16[1024,2048]{1,0:T(8,128)(2,1)}) custom-call(bf16[1280,256]{1,0:T(8,128)(2,1)S(1)} %collective-permute-done.5.a_ref.refs_0_, bf16[768,256]{1,0:T(8,128)(2,1)S(1)} %collective-permute-done.1.b_ref.refs_1_, ...), custom_call_target="tpu_custom_call", output_to_operand_aliasing={{0}: (5, {}), {1}: (6, {})} | custom-call | flops 3407872 | bytes 6815744 | tf_op jit(solution)/shard_map/place/pallas_call | solution.py:159
  125.0 0.9 place.7
  (4 shorter events, 0.1 us)
Async XLA Ops:
  0.6 1.2 copy-start
  0.6 1.5 %copy-start.1 = (f32[1,256,1024]{2,1,0:T(8,128)S(1)}, f32[1,256,1024]{2,1,0:T(8,128)}, u32[]{:S(2)}) copy-start(f32[1,256,1024]{2,1,0:T(8,128)} %param.8) | copy-start | bytes 3145732
  2.4 24.9 %collective-permute-start.3 = (bf16[1024,256]{1,0:T(8,128)(2,1)S(1)}, bf16[1024,256]{1,0:T(8,128)(2,1)S(1)}, u32[]{:S(2)}, u32[]{:S(2)}) collective-permute-start(bf16[1024,256]{1,0:T(8,128)(2,1)S(1)} %mix.3.before), channel_id=1, source_target_pairs={{0,6},{2,0},{4,2},{6,4},{256,258},{258,260},{260,262},{262,256},{1... | collective-permute-start | bytes 1572872 | tf_op jit(solution)/shard_map/ppermute | solution.py:213
  15.1 60.8 %copy-start.2 = (f32[256,1]{0,1:T(1,128)S(1)}, f32[256,1]{0,1:T(1,128)}, u32[]{:S(2)}) copy-start(f32[256,1]{0,1:T(1,128)} %param.12) | copy-start | bytes 3076
  15.1 60.8 %copy-start.3 = (f32[256]{0:T(256)S(1)}, f32[256]{0:T(256)}, u32[]{:S(2)}) copy-start(f32[256]{0:T(256)} %param.13) | copy-start | bytes 3076
  15.1 12.2 %collective-permute-start.4 = (bf16[256,256]{1,0:T(8,128)(2,1)S(1)}, bf16[256,256]{1,0:T(8,128)(2,1)S(1)}, u32[]{:S(2)}, u32[]{:S(2)}) collective-permute-start(bf16[256,256]{1,0:T(8,128)(2,1)S(1)} %get-tuple-element.17), channel_id=1, source_target_pairs={{0,6},{2,0},{4,2},{6,4},{256,258},{258,260},{260,262},{262,256},{1... | collective-permute-start | bytes 393224 | tf_op jit(solution)/shard_map/ppermute | solution.py:213
  27.3 33.4 %collective-permute-start.5 = (bf16[1280,256]{1,0:T(8,128)(2,1)S(1)}, bf16[1280,256]{1,0:T(8,128)(2,1)S(1)}, u32[]{:S(2)}, u32[]{:S(2)}) collective-permute-start(bf16[1280,256]{1,0:T(8,128)(2,1)S(1)} %join.3.a_ref.refs_0_), channel_id=1, source_target_pairs={{0,6},{2,0},{4,2},{6,4},{256,258},{258,260},{260,262},{262,256},{1... | collective-permute-start | bytes 1966088 | tf_op jit(solution)/shard_map/ppermute | solution.py:213
  36.0 18.5 %collective-permute-start = (bf16[768,256]{1,0:T(8,128)(2,1)S(1)}, bf16[768,256]{1,0:T(8,128)(2,1)S(1)}, u32[]{:S(2)}, u32[]{:S(2)}) collective-permute-start(bf16[768,256]{1,0:T(8,128)(2,1)S(1)} %get-tuple-element.16), channel_id=1, source_target_pairs={{0,6},{2,0},{4,2},{6,4},{256,258},{258,260},{260,262},{262,256},{1... | collective-permute-start | bytes 1179656 | tf_op jit(solution)/shard_map/ppermute | solution.py:213
  54.5 15.7 %collective-permute-start.1 = (bf16[768,256]{1,0:T(8,128)(2,1)S(1)}, bf16[768,256]{1,0:T(8,128)(2,1)S(1)}, u32[]{:S(2)}, u32[]{:S(2)}) collective-permute-start(bf16[768,256]{1,0:T(8,128)(2,1)S(1)} %collective-permute-done.b_ref.refs_1_), channel_id=1, source_target_pairs={{0,6},{2,0},{4,2},{6,4},{256,258},{258,260},{260,262},{262,256},{1... | collective-permute-start | bytes 1179656 | tf_op jit(solution)/shard_map/ppermute | solution.py:213
  60.7 38.4 %collective-permute-start.7 = (bf16[1280,256]{1,0:T(8,128)(2,1)S(1)}, bf16[1280,256]{1,0:T(8,128)(2,1)}, u32[]{:S(2)}, u32[]{:S(2)}) collective-permute-start(bf16[1280,256]{1,0:T(8,128)(2,1)S(1)} %collective-permute-done.5.a_ref.refs_0_), channel_id=1, source_target_pairs={{0,6},{2,0},{4,2},{6,4},{256,258},{258,260},{260,262},{262,256},{1... | collective-permute-start | bytes 1966088 | tf_op jit(solution)/shard_map/ppermute | solution.py:213
  62.7 56.0 %collective-permute-start.9 = (bf16[2048,256]{1,0:T(8,128)(2,1)}, bf16[2048,256]{1,0:T(8,128)(2,1)}, u32[]{:S(2)}, u32[]{:S(2)}) collective-permute-start(bf16[2048,256]{1,0:T(8,128)(2,1)} %get-tuple-element.18.refs_0_), channel_id=1, source_target_pairs={{0,1},{1,0},{2,3},{3,2},{4,5},{5,4},{6,7},{7,6},{8,9},{9,8},{10,11... | collective-permute-start | bytes 3145736 | tf_op jit(solution)/shard_map/ppermute | solution.py:216
  68.3 50.3 %collective-permute-start.10 = (bf16[2048,256]{1,0:T(8,128)(2,1)}, bf16[2048,256]{1,0:T(8,128)(2,1)}, u32[]{:S(2)}, u32[]{:S(2)}) collective-permute-start(bf16[2048,256]{1,0:T(8,128)(2,1)} %join.5), channel_id=1, source_target_pairs={{0,1},{1,0},{2,3},{3,2},{4,5},{5,4},{6,7},{7,6},{8,9},{9,8},{10,11... | collective-permute-start | bytes 3145736 | tf_op jit(solution)/shard_map/ppermute | solution.py:216
  71.3 50.6 %collective-permute-start.6 = (bf16[2048,256]{1,0:T(8,128)(2,1)}, bf16[2048,256]{1,0:T(8,128)(2,1)S(1)}, u32[]{:S(2)}, u32[]{:S(2)}) collective-permute-start(bf16[2048,256]{1,0:T(8,128)(2,1)} %join.4), channel_id=1, source_target_pairs={{0,1},{1,0},{2,3},{3,2},{4,5},{5,4},{6,7},{7,6},{8,9},{9,8},{10,11... | collective-permute-start | bytes 3145736 | tf_op jit(solution)/shard_map/ppermute | solution.py:216
  89.4 21.0 %all-to-all-start.1 = ((bf16[32,32,128]{2,1,0:T(8,128)(2,1)}), bf16[32,32,128]{2,1,0:T(8,128)(2,1)S(1)}, u32[]{:S(2)}, u32[]{:S(2)}) async-start(bf16[32,32,128]{2,1,0:T(8,128)(2,1)} %broadcast_in_dim.29), calls=%async_computation.1 | async-start | bytes 524288 | tf_op jit(solution)/shard_map/all_to_all | solution.py:201
  99.1 22.8 %collective-permute-start.8 = (bf16[1280,256]{1,0:T(8,128)(2,1)}, bf16[1280,256]{1,0:T(8,128)(2,1)}, u32[]{:S(2)}, u32[]{:S(2)}) collective-permute-start(bf16[1280,256]{1,0:T(8,128)(2,1)} %collective-permute-done.7.refs_3_), channel_id=1, source_target_pairs={{0,1},{1,0},{2,3},{3,2},{4,5},{5,4},{6,7},{7,6},{8,9},{9,8},{10,11... | collective-permute-start | bytes 1966088 | tf_op jit(solution)/shard_map/ppermute | solution.py:216
  102.0 13.6 %collective-permute-start.2 = (bf16[768,256]{1,0:T(8,128)(2,1)S(1)}, bf16[768,256]{1,0:T(8,128)(2,1)}, u32[]{:S(2)}, u32[]{:S(2)}) collective-permute-start(bf16[768,256]{1,0:T(8,128)(2,1)S(1)} %collective-permute-done.1.b_ref.refs_1_), channel_id=1, source_target_pairs={{0,6},{2,0},{4,2},{6,4},{256,258},{258,260},{260,262},{262,256},{1... | collective-permute-start | bytes 1179656 | tf_op jit(solution)/shard_map/ppermute | solution.py:213
where the time goes:
time: 127 us; the launch traced here: 126 us
  starting transfers between devices  55.7 us (44%)
  waiting for transfers between devices  34.6 us (27%)
  Pallas kernels  16.6 us (13%)
  blocking collectives  15.9 us (13%)
  between operations  1.67 us (1%)
  local copies, waits for them, and re-layouts  1.5 us (1%)
    ppermute x7, starting transfers between devices, moved(): return lax.ppermute(x, ('zlo', 'zhi'), pairs)  32.1 us
    ppermute x7, waiting for transfers between devices, moved(): return lax.ppermute(x, ('zlo', 'zhi'), pairs)  30.6 us
    ppermute x4, starting transfers between devices, partner(): return lax.ppermute(x, 'core', [(0, 1), (1, 0)])  13.9 us
    all_to_all x1, blocking collectives, spread(): lax.all_to_all(jnp.broadcast_to(x[None], (n, *x.shape)), axes, 0, 0, tile...  12.8 us
    all_to_all x1, starting transfers between devices, spread(): lax.all_to_all(jnp.broadcast_to(x[None], (n, *x.shape)), axes, 0, 0, tile...  9.67 us
    pallas_call x4, Pallas kernels, placed(): pl.pallas_call(functools.partial(place_kernel, counts, by), out_shape=(ou...  9.5 us
    all_to_all x1, waiting for transfers between devices, spread(): lax.all_to_all(jnp.broadcast_to(x[None], (n, *x.shape)), axes, 0, 0, tile...  3.99 us
    pallas_call x2, Pallas kernels, mixed(): pl.pallas_call(functools.partial(mix_kernel, first, size), out_shape=(plt...  3.67 us
  transfers between devices with their start and end apart: 12, of which 4 were waited for; matrix products, arithmetic and copies ran while one was open for 1% of the time, Pallas kernels for 10%

commit v1 on v0

--- a/solution.py
+++ b/solution.py
@@ -244,11 +244,17 @@
     part = spread(part, ("y", "x")).reshape(-1, lanes)
     serve_router = ordered(part, nx * ny, nz).T
 
-    outs = place(None, (own, head(0, 0) + tail(0, 0)))
     d0 = partner(own)
     both = joined(a1, a2)
     d1 = partner(both)
-    outs = place(outs, (a1, head(1, 0)), (a2, tail(1, 0)), (d0, head(0, 1) + tail(0, 1)), (d1, head(1, 1) + tail(1, 1)))
+    outs = place(
+        None,
+        (own, head(0, 0) + tail(0, 0)),
+        (a1, head(1, 0)),
+        (a2, tail(1, 0)),
+        (d0, head(0, 1) + tail(0, 1)),
+        (d1, head(1, 1) + tail(1, 1)),
+    )
     both = joined(c1, c2)
     d2 = partner(both)
     outs = place(

time: 127 us -> 127 us (level)
  waiting for transfers between devices: 34.6 us -> 36.8 us
  Pallas kernels: 16.6 us -> 15 us
    all_to_all x1, waiting for transfers between devices: 3.99 us -> 6.21 us  [spread(): lax.all_to_all(jnp.broadcast_to(x[None], (n, *x.shape)), axes, 0, 0, tile...]
    pallas_call x4 -> x3, Pallas kernels: 9.5 us -> 7.98 us  [placed(): pl.pallas_call(functools.partial(place_kernel, counts, by), out_shape=(ou...]
  transfers between devices with their start and end apart: 12 -> 12, of which waited for: 4 -> 4; matrix products, arithmetic and copies ran while one was open for 1% -> 1% of each run, Pallas kernels for 10% -> 8%
where the time goes in v1:
time: 127 us
  starting transfers between devices  55.7 us (44%)
  waiting for transfers between devices  36.8 us (29%)
  blocking collectives  15.9 us (13%)
  Pallas kernels  15 us (12%)
  between operations  1.67 us (1%)
  local copies, waits for them, and re-layouts  1.5 us (1%)
    ppermute x7, starting transfers between devices, moved(): return lax.ppermute(x, ('zlo', 'zhi'), pairs)  32.1 us
    ppermute x7, waiting for transfers between devices, moved(): return lax.ppermute(x, ('zlo', 'zhi'), pairs)  30.6 us
    ppermute x4, starting transfers between devices, partner(): return lax.ppermute(x, 'core', [(0, 1), (1, 0)])  13.9 us
    all_to_all x1, blocking collectives, spread(): lax.all_to_all(jnp.broadcast_to(x[None], (n, *x.shape)), axes, 0, 0, tile...  12.8 us
    all_to_all x1, starting transfers between devices, spread(): lax.all_to_all(jnp.broadcast_to(x[None], (n, *x.shape)), axes, 0, 0, tile...  9.67 us
    pallas_call x3, Pallas kernels, placed(): pl.pallas_call(functools.partial(place_kernel, counts, by), out_shape=(ou...  7.98 us
    all_to_all x1, waiting for transfers between devices, spread(): lax.all_to_all(jnp.broadcast_to(x[None], (n, *x.shape)), axes, 0, 0, tile...  6.21 us
    pallas_call x2, Pallas kernels, mixed(): pl.pallas_call(functools.partial(mix_kernel, first, size), out_shape=(plt...  3.66 us
  transfers between devices with their start and end apart: 12, of which 4 were waited for; matrix products, arithmetic and copies ran while one was open for 1% of the time, Pallas kernels for 8%

profile of v1, /device:TPU:1, one launch (start us, length us, event | category | flops | bytes accessed | tf_op | source)
XLA Modules:
  0.0 126.6 jit_solution(17499100466087742937)
XLA Ops:
  0.6 0.0 copy-start
  0.6 0.0 copy-start.1
  1.5 0.4 copy-done
  1.9 0.3 copy-done.1
  2.2 0.2 mix.3.before
  2.4 11.5 %collective-permute-start.3 = (bf16[1024,256]{1,0:T(8,128)(2,1)S(1)}, bf16[1024,256]{1,0:T(8,128)(2,1)S(1)}, u32[]{:S(2)}, u32[]{:S(2)}) collective-permute-start(bf16[1024,256]{1,0:T(8,128)(2,1)S(1)} %mix.3.before), channel_id=1, source_target_pairs={{0,6},{2,0},{4,2},{6,4},{256,258},{258,260},{260,262},{262,256},{1... | collective-permute-start | bytes 1572872 | tf_op jit(solution)/shard_map/ppermute | solution.py:213
  13.9 1.2 mix.4
  15.1 0.0 copy-start.2
  15.1 0.0 copy-start.3
  15.1 2.2 %collective-permute-start.4 = (bf16[256,256]{1,0:T(8,128)(2,1)S(1)}, bf16[256,256]{1,0:T(8,128)(2,1)S(1)}, u32[]{:S(2)}, u32[]{:S(2)}) collective-permute-start(bf16[256,256]{1,0:T(8,128)(2,1)S(1)} %get-tuple-element.15), channel_id=1, source_target_pairs={{0,6},{2,0},{4,2},{6,4},{256,258},{258,260},{260,262},{262,256},{1... | collective-permute-start | bytes 393224 | tf_op jit(solution)/shard_map/ppermute | solution.py:213
  17.3 10.0 %collective-permute-done.4.b_ref = bf16[256,256]{1,0:T(8,128)(2,1)S(1)} collective-permute-done((bf16[256,256]{1,0:T(8,128)(2,1)S(1)}, bf16[256,256]{1,0:T(8,128)(2,1)S(1)}, u32[]{:S(2)}, u32[]{:S(2)}) %collective-permute-start.4) | collective-permute-done | bytes 131104 | tf_op jit(solution)/shard_map/ppermute | solution.py:213
  27.3 0.0 collective-permute-done.3.a_ref
  27.3 6.2 %collective-permute-start.5 = (bf16[1280,256]{1,0:T(8,128)(2,1)S(1)}, bf16[1280,256]{1,0:T(8,128)(2,1)S(1)}, u32[]{:S(2)}, u32[]{:S(2)}) collective-permute-start(bf16[1280,256]{1,0:T(8,128)(2,1)S(1)} %join.3.a_ref.refs_1_), channel_id=1, source_target_pairs={{0,6},{2,0},{4,2},{6,4},{256,258},{258,260},{260,262},{262,256},{1... | collective-permute-start | bytes 1966088 | tf_op jit(solution)/shard_map/ppermute | solution.py:213
  33.5 2.5 %mix.5 = (bf16[768,256]{1,0:T(8,128)(2,1)S(1)}, bf16[2048,256]{1,0:T(8,128)(2,1)}) custom-call(f32[1]{0:T(128)S(6)} %copy.18.share_ref, f32[256,1024]{1,0:T(8,128)} %bitcast.17, f32[256,1024]{1,0:T(8,128)} %bitcast.19, bf16[1280,256]{1,0:T(8,128)(2,1)S(1)} %get-tuple-element.13.before), custom_call_target="tpu_custom_call" | custom-call | flops 786432 | bytes 1966080 | tf_op jit(solution)/shard_map/mix/pallas_call | solution.py:91
  36.0 1.9 %collective-permute-start = (bf16[768,256]{1,0:T(8,128)(2,1)S(1)}, bf16[768,256]{1,0:T(8,128)(2,1)S(1)}, u32[]{:S(2)}, u32[]{:S(2)}) collective-permute-start(bf16[768,256]{1,0:T(8,128)(2,1)S(1)} %get-tuple-element.14), channel_id=1, source_target_pairs={{0,6},{2,0},{4,2},{6,4},{256,258},{258,260},{260,262},{262,256},{1... | collective-permute-start | bytes 1179656 | tf_op jit(solution)/shard_map/ppermute | solution.py:213
  38.0 16.5 %collective-permute-done.b_ref.refs_2_ = bf16[768,256]{1,0:T(8,128)(2,1)S(1)} collective-permute-done((bf16[768,256]{1,0:T(8,128)(2,1)S(1)}, bf16[768,256]{1,0:T(8,128)(2,1)S(1)}, u32[]{:S(2)}, u32[]{:S(2)}) %collective-permute-start) | collective-permute-done | bytes 393248 | tf_op jit(solution)/shard_map/ppermute | solution.py:213
  54.5 6.2 %collective-permute-start.1 = (bf16[768,256]{1,0:T(8,128)(2,1)S(1)}, bf16[768,256]{1,0:T(8,128)(2,1)S(1)}, u32[]{:S(2)}, u32[]{:S(2)}) collective-permute-start(bf16[768,256]{1,0:T(8,128)(2,1)S(1)} %collective-permute-done.b_ref.refs_2_), channel_id=1, source_target_pairs={{0,6},{2,0},{4,2},{6,4},{256,258},{258,260},{260,262},{262,256},{1... | collective-permute-start | bytes 1179656 | tf_op jit(solution)/shard_map/ppermute | solution.py:213
  60.7 0.0 collective-permute-done.5.a_ref.refs_0_
  60.7 1.9 %collective-permute-start.7 = (bf16[1280,256]{1,0:T(8,128)(2,1)S(1)}, bf16[1280,256]{1,0:T(8,128)(2,1)}, u32[]{:S(2)}, u32[]{:S(2)}) collective-permute-start(bf16[1280,256]{1,0:T(8,128)(2,1)S(1)} %collective-permute-done.5.a_ref.refs_0_), channel_id=1, source_target_pairs={{0,6},{2,0},{4,2},{6,4},{256,258},{258,260},{260,262},{262,256},{1... | collective-permute-start | bytes 1966088 | tf_op jit(solution)/shard_map/ppermute | solution.py:213
  62.7 4.6 %collective-permute-start.9 = (bf16[2048,256]{1,0:T(8,128)(2,1)}, bf16[2048,256]{1,0:T(8,128)(2,1)}, u32[]{:S(2)}, u32[]{:S(2)}) collective-permute-start(bf16[2048,256]{1,0:T(8,128)(2,1)} %get-tuple-element.16.refs_0_), channel_id=1, source_target_pairs={{0,1},{1,0},{2,3},{3,2},{4,5},{5,4},{6,7},{7,6},{8,9},{9,8},{10,11... | collective-permute-start | bytes 3145736 | tf_op jit(solution)/shard_map/ppermute | solution.py:216
  67.2 1.0 join.5
  68.3 1.9 %collective-permute-start.10 = (bf16[2048,256]{1,0:T(8,128)(2,1)}, bf16[2048,256]{1,0:T(8,128)(2,1)}, u32[]{:S(2)}, u32[]{:S(2)}) collective-permute-start(bf16[2048,256]{1,0:T(8,128)(2,1)} %join.5), channel_id=1, source_target_pairs={{0,1},{1,0},{2,3},{3,2},{4,5},{5,4},{6,7},{7,6},{8,9},{9,8},{10,11... | collective-permute-start | bytes 3145736 | tf_op jit(solution)/shard_map/ppermute | solution.py:216
  70.2 0.0 collective-permute-done.1.b_ref.refs_1_
  70.2 1.1 join.4
  71.3 4.5 %collective-permute-start.6 = (bf16[2048,256]{1,0:T(8,128)(2,1)}, bf16[2048,256]{1,0:T(8,128)(2,1)S(1)}, u32[]{:S(2)}, u32[]{:S(2)}) collective-permute-start(bf16[2048,256]{1,0:T(8,128)(2,1)} %join.4), channel_id=1, source_target_pairs={{0,1},{1,0},{2,3},{3,2},{4,5},{5,4},{6,7},{7,6},{8,9},{9,8},{10,11... | collective-permute-start | bytes 3145736 | tf_op jit(solution)/shard_map/ppermute | solution.py:216
  75.8 0.0 copy-done.2
  75.8 0.0 copy-done.3
  75.9 12.8 %all_to_all.10 = bf16[16,2,128]{2,1,0:T(2,128)(2,1)S(1)} all-to-all(bf16[16,2,128]{2,1,0:T(2,128)(2,1)S(1)} %broadcast_in_dim.27), channel_id=1, replica_groups=mesh['zlo'=2,'y'=8,'x'=4,'zhi'=4,'core'=2] {'zlo','zhi','core'}, dimensions={0} | all-to-all | bytes 16384 | tf_op jit(solution)/shard_map/all_to_all | solution.py:201
  88.7 0.7 broadcast_in_dim.29
  89.4 9.7 %all-to-all-start.1 = ((bf16[32,32,128]{2,1,0:T(8,128)(2,1)}), bf16[32,32,128]{2,1,0:T(8,128)(2,1)S(1)}, u32[]{:S(2)}, u32[]{:S(2)}) async-start(bf16[32,32,128]{2,1,0:T(8,128)(2,1)} %broadcast_in_dim.29), calls=%async_computation.1 | async-start | bytes 524288 | tf_op jit(solution)/shard_map/all_to_all | solution.py:201
  99.1 0.0 collective-permute-done.7.refs_3_
  99.1 2.8 %collective-permute-start.8 = (bf16[1280,256]{1,0:T(8,128)(2,1)}, bf16[1280,256]{1,0:T(8,128)(2,1)}, u32[]{:S(2)}, u32[]{:S(2)}) collective-permute-start(bf16[1280,256]{1,0:T(8,128)(2,1)} %collective-permute-done.7.refs_3_), channel_id=1, source_target_pairs={{0,1},{1,0},{2,3},{3,2},{4,5},{5,4},{6,7},{7,6},{8,9},{9,8},{10,11... | collective-permute-start | bytes 1966088 | tf_op jit(solution)/shard_map/ppermute | solution.py:216
  102.0 2.2 %collective-permute-start.2 = (bf16[768,256]{1,0:T(8,128)(2,1)S(1)}, bf16[768,256]{1,0:T(8,128)(2,1)}, u32[]{:S(2)}, u32[]{:S(2)}) collective-permute-start(bf16[768,256]{1,0:T(8,128)(2,1)S(1)} %collective-permute-done.1.b_ref.refs_1_), channel_id=1, source_target_pairs={{0,6},{2,0},{4,2},{6,4},{256,258},{258,260},{260,262},{262,256},{1... | collective-permute-start | bytes 1179656 | tf_op jit(solution)/shard_map/ppermute | solution.py:213
  104.2 6.2 %all-to-all-done.1 = bf16[32,32,128]{2,1,0:T(8,128)(2,1)S(1)} async-done(((bf16[32,32,128]{2,1,0:T(8,128)(2,1)}), bf16[32,32,128]{2,1,0:T(8,128)(2,1)S(1)}, u32[]{:S(2)}, u32[]{:S(2)}) %all-to-all-start.1) | async-done | bytes 262176 | tf_op jit(solution)/shard_map/all_to_all | solution.py:201
  110.4 1.0 order.1
  111.5 4.1 %collective-permute-done.2 = bf16[768,256]{1,0:T(8,128)(2,1)} collective-permute-done((bf16[768,256]{1,0:T(8,128)(2,1)S(1)}, bf16[768,256]{1,0:T(8,128)(2,1)}, u32[]{:S(2)}, u32[]{:S(2)}) %collective-permute-start.2) | collective-permute-done | bytes 393248 | tf_op jit(solution)/shard_map/ppermute | solution.py:213
  115.5 3.1 %all_gather.3.refs_0_ = bf16[1536,256]{1,0:T(8,128)(2,1)S(1)} all-gather(bf16[768,256]{1,0:T(8,128)(2,1)} %collective-permute-done.2), channel_id=1, replica_groups=mesh['zlo'=2,'y'=8,'x'=4,'zhi'=4,'core'=2] {'core'}, dimensions={0}, use_global_device_ids=true | all-gather | bytes 1179648 | tf_op jit(solution)/shard_map/all_gather | solution.py:268
  118.6 0.0 collective-permute-done.9.refs_3_
  118.6 0.0 collective-permute-done.10.refs_4_
  118.6 4.0 %place.3 = (bf16[1024,2048]{1,0:T(8,128)(2,1)}, bf16[1024,2048]{1,0:T(8,128)(2,1)}) custom-call(bf16[2048,256]{1,0:T(8,128)(2,1)} %get-tuple-element.16.refs_0_, bf16[1280,256]{1,0:T(8,128)(2,1)S(1)} %join.3.a_ref.refs_1_, bf16[768,256]{1,0:T(8,128)(2,1)S(1)} %collective-permute-done.b_ref.refs_2_, bf16[2048,256]{1,0:T(8,128)(2,1)} %collective-permute-done.9.refs_3_, ...), custom_call_target="tpu_custom_call" | custom-call | flops 4194304 | bytes 8388608 | tf_op jit(solution)/shard_map/place/pallas_call | solution.py:159
  122.6 0.0 collective-permute-done.6.refs_2_
  122.6 0.0 collective-permute-done.8.refs_4_
  122.6 3.1 %place.4 = (bf16[1024,2048]{1,0:T(8,128)(2,1)}, bf16[1024,2048]{1,0:T(8,128)(2,1)}) custom-call(bf16[1280,256]{1,0:T(8,128)(2,1)S(1)} %collective-permute-done.5.a_ref.refs_0_, bf16[768,256]{1,0:T(8,128)(2,1)S(1)} %collective-permute-done.1.b_ref.refs_1_, ...), custom_call_target="tpu_custom_call", output_to_operand_aliasing={{0}: (5, {}), {1}: (6, {})} | custom-call | flops 3407872 | bytes 6815744 | tf_op jit(solution)/shard_map/place/pallas_call | solution.py:159
  125.7 0.9 place.5
  (4 shorter events, 0.1 us)
Async XLA Ops:
  0.6 1.2 copy-start
  0.6 1.5 %copy-start.1 = (f32[1,256,1024]{2,1,0:T(8,128)S(1)}, f32[1,256,1024]{2,1,0:T(8,128)}, u32[]{:S(2)}) copy-start(f32[1,256,1024]{2,1,0:T(8,128)} %param.8) | copy-start | bytes 3145732
  2.4 24.9 %collective-permute-start.3 = (bf16[1024,256]{1,0:T(8,128)(2,1)S(1)}, bf16[1024,256]{1,0:T(8,128)(2,1)S(1)}, u32[]{:S(2)}, u32[]{:S(2)}) collective-permute-start(bf16[1024,256]{1,0:T(8,128)(2,1)S(1)} %mix.3.before), channel_id=1, source_target_pairs={{0,6},{2,0},{4,2},{6,4},{256,258},{258,260},{260,262},{262,256},{1... | collective-permute-start | bytes 1572872 | tf_op jit(solution)/shard_map/ppermute | solution.py:213
  15.1 60.8 %copy-start.2 = (f32[256,1]{0,1:T(1,128)S(1)}, f32[256,1]{0,1:T(1,128)}, u32[]{:S(2)}) copy-start(f32[256,1]{0,1:T(1,128)} %param.12) | copy-start | bytes 3076
  15.1 60.8 %copy-start.3 = (f32[256]{0:T(256)S(1)}, f32[256]{0:T(256)}, u32[]{:S(2)}) copy-start(f32[256]{0:T(256)} %param.13) | copy-start | bytes 3076
  15.1 12.2 %collective-permute-start.4 = (bf16[256,256]{1,0:T(8,128)(2,1)S(1)}, bf16[256,256]{1,0:T(8,128)(2,1)S(1)}, u32[]{:S(2)}, u32[]{:S(2)}) collective-permute-start(bf16[256,256]{1,0:T(8,128)(2,1)S(1)} %get-tuple-element.15), channel_id=1, source_target_pairs={{0,6},{2,0},{4,2},{6,4},{256,258},{258,260},{260,262},{262,256},{1... | collective-permute-start | bytes 393224 | tf_op jit(solution)/shard_map/ppermute | solution.py:213
  27.3 33.4 %collective-permute-start.5 = (bf16[1280,256]{1,0:T(8,128)(2,1)S(1)}, bf16[1280,256]{1,0:T(8,128)(2,1)S(1)}, u32[]{:S(2)}, u32[]{:S(2)}) collective-permute-start(bf16[1280,256]{1,0:T(8,128)(2,1)S(1)} %join.3.a_ref.refs_1_), channel_id=1, source_target_pairs={{0,6},{2,0},{4,2},{6,4},{256,258},{258,260},{260,262},{262,256},{1... | collective-permute-start | bytes 1966088 | tf_op jit(solution)/shard_map/ppermute | solution.py:213
  36.0 18.5 %collective-permute-start = (bf16[768,256]{1,0:T(8,128)(2,1)S(1)}, bf16[768,256]{1,0:T(8,128)(2,1)S(1)}, u32[]{:S(2)}, u32[]{:S(2)}) collective-permute-start(bf16[768,256]{1,0:T(8,128)(2,1)S(1)} %get-tuple-element.14), channel_id=1, source_target_pairs={{0,6},{2,0},{4,2},{6,4},{256,258},{258,260},{260,262},{262,256},{1... | collective-permute-start | bytes 1179656 | tf_op jit(solution)/shard_map/ppermute | solution.py:213
  54.5 15.7 %collective-permute-start.1 = (bf16[768,256]{1,0:T(8,128)(2,1)S(1)}, bf16[768,256]{1,0:T(8,128)(2,1)S(1)}, u32[]{:S(2)}, u32[]{:S(2)}) collective-permute-start(bf16[768,256]{1,0:T(8,128)(2,1)S(1)} %collective-permute-done.b_ref.refs_2_), channel_id=1, source_target_pairs={{0,6},{2,0},{4,2},{6,4},{256,258},{258,260},{260,262},{262,256},{1... | collective-permute-start | bytes 1179656 | tf_op jit(solution)/shard_map/ppermute | solution.py:213
  60.7 38.4 %collective-permute-start.7 = (bf16[1280,256]{1,0:T(8,128)(2,1)S(1)}, bf16[1280,256]{1,0:T(8,128)(2,1)}, u32[]{:S(2)}, u32[]{:S(2)}) collective-permute-start(bf16[1280,256]{1,0:T(8,128)(2,1)S(1)} %collective-permute-done.5.a_ref.refs_0_), channel_id=1, source_target_pairs={{0,6},{2,0},{4,2},{6,4},{256,258},{258,260},{260,262},{262,256},{1... | collective-permute-start | bytes 1966088 | tf_op jit(solution)/shard_map/ppermute | solution.py:213
  62.7 56.0 %collective-permute-start.9 = (bf16[2048,256]{1,0:T(8,128)(2,1)}, bf16[2048,256]{1,0:T(8,128)(2,1)}, u32[]{:S(2)}, u32[]{:S(2)}) collective-permute-start(bf16[2048,256]{1,0:T(8,128)(2,1)} %get-tuple-element.16.refs_0_), channel_id=1, source_target_pairs={{0,1},{1,0},{2,3},{3,2},{4,5},{5,4},{6,7},{7,6},{8,9},{9,8},{10,11... | collective-permute-start | bytes 3145736 | tf_op jit(solution)/shard_map/ppermute | solution.py:216
  68.3 50.3 %collective-permute-start.10 = (bf16[2048,256]{1,0:T(8,128)(2,1)}, bf16[2048,256]{1,0:T(8,128)(2,1)}, u32[]{:S(2)}, u32[]{:S(2)}) collective-permute-start(bf16[2048,256]{1,0:T(8,128)(2,1)} %join.5), channel_id=1, source_target_pairs={{0,1},{1,0},{2,3},{3,2},{4,5},{5,4},{6,7},{7,6},{8,9},{9,8},{10,11... | collective-permute-start | bytes 3145736 | tf_op jit(solution)/shard_map/ppermute | solution.py:216
  71.3 51.3 %collective-permute-start.6 = (bf16[2048,256]{1,0:T(8,128)(2,1)}, bf16[2048,256]{1,0:T(8,128)(2,1)S(1)}, u32[]{:S(2)}, u32[]{:S(2)}) collective-permute-start(bf16[2048,256]{1,0:T(8,128)(2,1)} %join.4), channel_id=1, source_target_pairs={{0,1},{1,0},{2,3},{3,2},{4,5},{5,4},{6,7},{7,6},{8,9},{9,8},{10,11... | collective-permute-start | bytes 3145736 | tf_op jit(solution)/shard_map/ppermute | solution.py:216
  89.4 21.0 %all-to-all-start.1 = ((bf16[32,32,128]{2,1,0:T(8,128)(2,1)}), bf16[32,32,128]{2,1,0:T(8,128)(2,1)S(1)}, u32[]{:S(2)}, u32[]{:S(2)}) async-start(bf16[32,32,128]{2,1,0:T(8,128)(2,1)} %broadcast_in_dim.29), calls=%async_computation.1 | async-start | bytes 524288 | tf_op jit(solution)/shard_map/all_to_all | solution.py:201
  99.1 23.5 %collective-permute-start.8 = (bf16[1280,256]{1,0:T(8,128)(2,1)}, bf16[1280,256]{1,0:T(8,128)(2,1)}, u32[]{:S(2)}, u32[]{:S(2)}) collective-permute-start(bf16[1280,256]{1,0:T(8,128)(2,1)} %collective-permute-done.7.refs_3_), channel_id=1, source_target_pairs={{0,1},{1,0},{2,3},{3,2},{4,5},{5,4},{6,7},{7,6},{8,9},{9,8},{10,11... | collective-permute-start | bytes 1966088 | tf_op jit(solution)/shard_map/ppermute | solution.py:216
  102.0 13.6 %collective-permute-start.2 = (bf16[768,256]{1,0:T(8,128)(2,1)S(1)}, bf16[768,256]{1,0:T(8,128)(2,1)}, u32[]{:S(2)}, u32[]{:S(2)}) collective-permute-start(bf16[768,256]{1,0:T(8,128)(2,1)S(1)} %collective-permute-done.1.b_ref.refs_1_), channel_id=1, source_target_pairs={{0,6},{2,0},{4,2},{6,4},{256,258},{258,260},{260,262},{262,256},{1... | collective-permute-start | bytes 1179656 | tf_op jit(solution)/shard_map/ppermute | solution.py:213
